TPU v7x, 8 devices: a whole 2x2x1 slice. The times are simulated.
8 devices in a mesh: dp: 1 (over z), tp: 2 (over y), ep: 4 (over x, core).
Axes of the slice: x: 2, y: 2, z: 1, core: 2. Of those that a mesh axis runs over, the one named last changes fastest.
Arguments:
- tokens_x: bfloat16 [1024, 2048], P(('dp', 'ep', 'tp'))
- expert_ids: int32 [1024, 2], P(('dp', 'ep', 'tp'))
- route_gate: float32 [1024, 2], P(('dp', 'ep', 'tp'))
- w_gate: bfloat16 [8, 2048, 5632], P('ep', None, 'tp')
- w_up: bfloat16 [8, 2048, 5632], P('ep', None, 'tp')
- w_down: bfloat16 [8, 5632, 2048], P('ep', 'tp')
Outputs:
- output: bfloat16 [1024, 2048], P(('dp', 'ep', 'tp'))
All inputs are finite; a program needn't handle non-finite values.
Results may differ from a plain program's by a relative error of at most 0.00124.
Values are sent between devices in bfloat16 or wider.
A program may use at most 1 GiB of HBM per device.

v0:
```python
import jax
import jax.numpy as jnp
from jax import lax
from jax.sharding import PartitionSpec as P, NamedSharding


def solution(mesh):
    ep_size = mesh.shape['ep']
    row_spec = P(('dp', 'ep', 'tp'), None)
    w_in_spec = P('ep', None, 'tp')
    w_out_spec = P('ep', 'tp', None)

    def local_moe(x_local, ids_local, gate_local, w_gate, w_up, w_down):
        e_local = w_gate.shape[0]
        x_all = lax.all_gather(x_local, ('ep', 'tp'), tiled=True)
        ids_all = lax.all_gather(ids_local, ('ep', 'tp'), tiled=True)
        gate_all = lax.all_gather(gate_local, ('ep', 'tp'), tiled=True)
        num_tok, top_k = ids_all.shape
        local_pairs = num_tok * top_k // ep_size
        expert_cap = local_pairs // e_local
        local_ids = ids_all.reshape(-1) - lax.axis_index('ep') * e_local
        is_local = (local_ids >= 0) & (local_ids < e_local)
        sort_order = jnp.argsort(jnp.where(is_local, local_ids, e_local), stable=True)[:local_pairs]
        tok_rows = sort_order // top_k
        gate_rows = gate_all.reshape(-1)[sort_order]
        x_rows = x_all[tok_rows].reshape(e_local, expert_cap, -1)
        h_gate = jnp.einsum('ecd,edf->ecf', x_rows, w_gate, preferred_element_type=jnp.float32)
        h_up = jnp.einsum('ecd,edf->ecf', x_rows, w_up, preferred_element_type=jnp.float32)
        hidden = (jax.nn.silu(h_gate) * h_up).astype(jnp.bfloat16)
        out_rows = jnp.einsum('ecf,efd->ecd', hidden, w_down, preferred_element_type=jnp.float32)
        out_rows = out_rows.reshape(local_pairs, -1) * gate_rows[:, None]
        partial_sum = jax.ops.segment_sum(out_rows, tok_rows, num_segments=num_tok)
        y_local = lax.psum_scatter(partial_sum, ('ep', 'tp'), scatter_dimension=0, tiled=True)
        return y_local.astype(jnp.bfloat16)

    return jax.shard_map(local_moe, mesh=mesh, in_specs=(row_spec, row_spec, row_spec, w_in_spec, w_in_spec, w_out_spec), out_specs=row_spec, check_vma=False)
```

profile of v0, /device:TPU:0, one launch (start us, length us, event | category | flops | bytes accessed | tf_op | source)
XLA Modules:
  0.0 173.8 jit_solution(15670074454687235127)
XLA Ops:
  6.5 0.0 all-gather.2.cloned.1.call-start
  6.5 0.7 all-gather.2.cloned.1.call-update
  7.3 0.0 reduce-scatter.2.cloned.1.call-start
  7.3 13.6 %all_gather.11 = f32[1024,2]{0,1:T(2,128)S(1)} all-gather(f32[128,2]{0,1:T(2,128)} %param.8), channel_id=1, replica_groups=mesh['dp'=1,'tp'=2,'ep'=4] {'ep','tp'}, dimensions={0}, use_global_device_ids=true | all-gather | bytes 9216 | tf_op jit(solution)/shard_map/all_gather | solution.py:17
  20.9 0.2 copy.8
  21.1 0.3 reshape.15
  21.4 10.8 %all_gather.9 = s32[1024,2]{0,1:T(2,128)S(1)} all-gather(s32[128,2]{0,1:T(2,128)} %param.7), channel_id=1, replica_groups=mesh['dp'=1,'tp'=2,'ep'=4] {'ep','tp'}, dimensions={0}, use_global_device_ids=true | all-gather | bytes 9216 | tf_op jit(solution)/shard_map/all_gather | solution.py:16
  32.2 0.2 copy.7
  32.4 0.3 sub.17
  32.7 5.0 %sort.17 = (s32[2048]{0:T(1024)}, s32[2048]{0:T(1024)S(1)}) sort(s32[2048]{0:T(1024)S(1)} %and_select_fusion, s32[2048]{0:T(1024)S(1)} %iota.4), dimensions={0}, to_apply=%region_0.1 | sort | flops 22528 | bytes 32768 | tf_op jit(solution)/shard_map/jit(argsort)/sort | solution.py:23
  37.8 3.1 %gather_fusion.1 = f32[512]{0:T(512)S(1)} fusion(f32[2048]{0:T(1024)S(1)} %reshape.15, s32[1024]{0:T(1024)S(1)} %pad_clamp_fusion), kind=kCustom, calls=%fused_computation.1 | custom fusion | bytes 6144 | tf_op jit(solution)/shard_map/gather | solution.py:25
  41.0 1.9 %all-gather.2.cloned.1.call-done = bf16[1024,2048]{1,0:T(8,128)(2,1)} async-done(((bf16[128,2048]{1,0:T(8,128)(2,1)}), bf16[1024,2048]{1,0:T(8,128)(2,1)}) %all-gather.2.cloned.1.call-update) | async-done | bytes 4194320 | tf_op jit(solution)/shard_map/all_gather | solution.py:15
  42.8 7.1 %gather_fusion = bf16[512,2048]{1,0:T(8,128)(2,1)S(1)} fusion(bf16[1024,2048]{1,0:T(8,128)(2,1)} %all-gather.2.cloned.1.call-done, s32[1024]{0:T(1024)S(1)} %pad_clamp_fusion.1), kind=kCustom, calls=%fused_computation | custom fusion | bytes 4196352 | tf_op jit(solution)/shard_map/gather | solution.py:26
  50.0 13.2 %fusion.7 = f32[2,256,2816]{2,1,0:T(8,128)} fusion(bf16[2,256,2048]{2,1,0:T(8,128)(2,1)S(1)} %bitcast.8, bf16[2,2048,2816]{2,1,0:T(8,128)(2,1)} %param.9), kind=kOutput, calls=%fused_computation.23 | convolution fusion | flops 5905580032 | bytes 30932992 | tf_op jit(solution)/shard_map/ecd,edf->ecf/dot_general | solution.py:27
  63.2 22.5 %fusion = f32[2,256,2048]{2,1,0:T(8,128)} fusion(bf16[2,2816,2048]{2,1,0:T(8,128)(2,1)} %param.11, f32[2,256,2816]{2,1,0:T(8,128)} %fusion.7, bf16[2,256,2048]{2,1,0:T(8,128)(2,1)S(1)} %bitcast.9, bf16[2,2048,2816]{2,1,0:T(8,128)(2,1)} %param.10), kind=kOutput, calls=%fused_computation.4 | convolution fusion | flops 11819810816 | bytes 58195968 | tf_op jit(solution)/shard_map/ecf,efd->ecd/dot_general | solution.py:30
  85.7 4.5 %bitcast_multiply_fusion = f32[512,2048]{1,0:T(8,128)} fusion(f32[2,256,2048]{2,1,0:T(8,128)} %fusion, f32[512]{0:T(512)S(1)} %gather_fusion.1), kind=kLoop, calls=%fused_computation.5 | loop fusion | flops 1048576 | bytes 8390656 | tf_op jit(solution)/shard_map/mul | solution.py:31
  90.2 12.3 %scatter_custom_fusion = f32[1024,2048]{1,0:T(8,128)} fusion(s32[512]{0:T(512)S(1)} %get-tuple-element.8, f32[512,2048]{1,0:T(8,128)} %bitcast_multiply_fusion, f32[]{:T(128)} %constant.10.clone.1), kind=kCustom, calls=%fused_computation.6 | custom fusion | flops 1048576 | bytes 8389120 | tf_op jit(solution)/shard_map/scatter-add | solution.py:32
  102.5 0.0 reduce-scatter.2.cloned.1.call-update
  102.5 62.4 %reduce-scatter.2.cloned.1.call-done = f32[128,2048]{1,0:T(8,128)} async-done(((f32[1024,2048]{1,0:T(8,128)}), f32[128,2048]{1,0:T(8,128)}) %reduce-scatter.2.cloned.1.call-update) | async-done | bytes 1048592 | tf_op jit(solution)/shard_map/reduce_scatter | solution.py:33
  164.9 2.1 %convert_element_type.7 = bf16[128,2048]{1,0:T(8,128)(2,1)} convert(f32[128,2048]{1,0:T(8,128)} %reduce-scatter.2.cloned.1.call-done) | non-fusion elementwise | flops 262144 | bytes 1572864 | tf_op jit(solution)/shard_map/convert_element_type | solution.py:34
  (6 shorter events, 0.0 us)
Async XLA Ops:
  6.5 36.3 %all-gather.2.cloned.1.call-start = ((), (), s32[]{:S(2)}) async-start(), calls=%async_computation.1 | async-start | bytes 4718592 | tf_op jit(solution)/shard_map/all_gather | solution.py:15
  7.3 157.6 %reduce-scatter.2.cloned.1.call-start = ((), (), s32[]{:S(2)}) async-start(), calls=%async_computation.2 | async-start | bytes 9437184 | tf_op jit(solution)/shard_map/reduce_scatter | solution.py:33
Sparse Core Ops, SparseCore 0:
  9.1 33.6 all-gather.1
  102.6 62.2 reduce-scatter.1
where the time goes:
time: 174 us
  waiting for transfers between devices  65 us (37%)
  matrix products  35.7 us (21%)
  blocking collectives  24.4 us (14%)
  other arithmetic  24 us (14%)
  between operations  13.5 us (8%)
  local copies, waits for them, and re-layouts  11.3 us (6%)
    reduce_scatter x1, waiting for transfers between devices, local_moe(): lax.psum_scatter(partial_sum, ('ep', 'tp'), scatter_dimension=0, tiled=True)  62.4 us
    dot_general x1, matrix products, local_moe(): jnp.einsum('ecf,efd->ecd', hidden, w_down, preferred_element_type=jnp.flo...  22.5 us
    all_gather x1, blocking collectives, local_moe(): gate_all = lax.all_gather(gate_local, ('ep', 'tp'), tiled=True)  13.6 us
    dot_general x1, matrix products, local_moe(): jnp.einsum('ecd,edf->ecf', x_rows, w_gate, preferred_element_type=jnp.flo...  13.2 us
    scatter-add x1, other arithmetic, local_moe(): partial_sum = jax.ops.segment_sum(out_rows, tok_rows, num_segments=num_tok)  12.3 us
    all_gather x1, blocking collectives, local_moe(): ids_all = lax.all_gather(ids_local, ('ep', 'tp'), tiled=True)  10.8 us
    gather x1, local copies, waits for them, and re-layouts, local_moe(): x_rows = x_all[tok_rows].reshape(e_local, expert_cap, -1)  7.13 us
    sort x1, other arithmetic, local_moe(): jnp.argsort(jnp.where(is_local, local_ids, e_local), stable=True)  5.04 us
  transfers between devices with their start and end apart: 2, of which 2 were waited for; matrix products, arithmetic and copies ran while one was open for 5% of the time, Pallas kernels for 0%

commit v1 on v0

v1 whole, which is shorter than its diff:
```python
import functools

import jax
import jax.numpy as jnp
from jax import lax
from jax.experimental import pallas as pl
from jax.experimental.pallas import tpu as pltpu
from jax.sharding import PartitionSpec as P

MESH = pl.DeviceIdType.MESH
BF16 = jnp.bfloat16
F32 = jnp.float32
CW = 256


def moe_kernel(ids_ref, gate_ref, x_ref, wg_hbm, wu_hbm, wd_hbm, y_ref,
               gbuf, ubuf, dbuf, xbuf, sendbuf, hbuf, obuf, ybuf, hy, hx, psend, precv, dacc,
               ids_p, gate_p, sel, gsel,
               gsem, usem, dsem, xs_sem, xr_sem, aux_s, aux_r,
               ys_sem, yr_sem, x1s_sem, x1r_sem, y2s_sem, y2r_sem, ps_sem, pr_sem):
    n_gu = gbuf.shape[0]
    n_cc = ybuf.shape[1]
    slots = sendbuf.shape[1]
    ep = lax.axis_index('ep')
    tp = lax.axis_index('tp')
    other_tp = 1 - tp
    me = tp * 4 + ep

    def dev(e, t):
        return {'ep': e, 'tp': t}

    peers = [(dt, de) for dt in (0, 1) for de in range(4) if (dt, de) != (0, 0)]

    def peer(dt, de):
        return lax.rem(ep + de, 4), lax.rem(tp + dt, 2)

    def gu_copy(p, j):
        cols = pl.ds(pl.multiple_of(j * CW, CW), CW)
        return (pltpu.make_async_copy(wg_hbm.at[p, :, cols], gbuf.at[j], gsem.at[j]),
                pltpu.make_async_copy(wu_hbm.at[p, :, cols], ubuf.at[j], usem.at[j]))

    def d_copy(p, c):
        cols = pl.ds(pl.multiple_of(c * CW, CW), CW)
        return pltpu.make_async_copy(wd_hbm.at[p, :, cols], dbuf.at[c], dsem.at[c])

    @pl.loop(0, n_gu)
    def _(j):
        a, b = gu_copy(0, j)
        a.start()
        b.start()

    @pl.loop(0, 2 * n_cc)
    def _(c):
        d_copy(0, c).start()

    barrier = pltpu.get_barrier_semaphore()
    for dt, de in peers:
        e, t = peer(dt, de)
        pl.semaphore_signal(barrier, inc=1, device_id=dev(e, t), device_id_type=MESH)

    def slot_of(ids):
        ids = ids[...]
        e_iota = lax.broadcasted_iota(jnp.int32, (16, 128), 0)
        one0 = jnp.where(e_iota == ids[0:1, :], 1.0, 0.0).astype(F32)
        one1 = jnp.where(e_iota == ids[1:2, :], 1.0, 0.0).astype(F32)
        before = jnp.where(lax.broadcasted_iota(jnp.int32, (128, 128), 0)
                           < lax.broadcasted_iota(jnp.int32, (128, 128), 1), 1.0, 0.0)
        count = jnp.dot((one0 + one1).astype(BF16), before.astype(BF16), preferred_element_type=F32)
        rank0 = jnp.sum(one0 * count, axis=0, keepdims=True).astype(jnp.int32)
        rank1 = jnp.sum(one1 * count, axis=0, keepdims=True).astype(jnp.int32)
        return ids[0:1, :] * slots + rank0, ids[1:2, :] * slots + rank1

    def build(which, ids, gates):
        pos0, pos1 = slot_of(ids)
        k_iota = lax.broadcasted_iota(jnp.int32, (8 * slots, 128), 0)
        hit0 = jnp.where(k_iota == pos0, 1.0, 0.0).astype(F32)
        hit1 = jnp.where(k_iota == pos1, 1.0, 0.0).astype(F32)
        picked = hit0 * gates[0:1, :] + hit1 * gates[1:2, :]
        gsel[which] = jnp.broadcast_to(jnp.sum(picked, axis=1, keepdims=True), (8 * slots, CW))
        both = hit0 + hit1
        sel[which] = both.T.astype(BF16)
        return both.astype(BF16)

    gather = build(0, ids_ref, gate_ref)
    sorted_rows = jnp.dot(gather, x_ref[...], preferred_element_type=F32).astype(BF16)
    sendbuf[...] = sorted_rows.reshape(sendbuf.shape)

    pl.semaphore_wait(barrier, 7)

    def aux_copies():
        return (pltpu.make_async_remote_copy(ids_ref, ids_p, aux_s.at[0], aux_r.at[0],
                                             device_id=dev(ep, other_tp), device_id_type=MESH),
                pltpu.make_async_remote_copy(gate_ref, gate_p, aux_s.at[1], aux_r.at[1],
                                             device_id=dev(ep, other_tp), device_id_type=MESH))

    for copy in aux_copies():
        copy.start()

    def row_copy(p, i, src_home):
        dt, de = peers[i]
        e, t = peer(dt, de)
        return pltpu.make_async_remote_copy(
            sendbuf.at[2 * e + p], xbuf.at[p, src_home], xs_sem.at[p, i], xr_sem.at[p, src_home],
            device_id=dev(e, t), device_id_type=MESH)

    for p in range(2):
        for i in range(7):
            row_copy(p, i, me).start()
        xbuf[p, me] = sendbuf[2 * ep + p]

    def o_view(p, c):
        return obuf.at[p, c]

    def y1_copy(p, cc):
        return pltpu.make_async_remote_copy(
            obuf.at[p, 2 * cc, other_tp], ybuf.at[p, cc], ys_sem.at[p, cc], yr_sem.at[p, cc],
            device_id=dev(ep, other_tp), device_id_type=MESH)

    def x1_copy(p, cc, de, src_ep):
        he = lax.rem(ep + de, 4)
        return pltpu.make_async_remote_copy(
            obuf.at[p, 2 * cc + 1, :, he], hx.at[cc, :, 2 * src_ep + p],
            x1s_sem.at[p, cc, de - 1], x1r_sem.at[p, cc, src_ep],
            device_id=dev(he, tp), device_id_type=MESH)

    def y2_copy(p, cc, de, src_ep):
        he = lax.rem(ep + de, 4)
        return pltpu.make_async_remote_copy(
            ybuf.at[p, cc, he], hy.at[cc, 2 * src_ep + p],
            y2s_sem.at[p, cc, de - 1], y2r_sem.at[p, cc, src_ep],
            device_id=dev(he, tp), device_id_type=MESH)

    def p_copy(cc):
        return pltpu.make_async_remote_copy(
            psend.at[cc], precv.at[cc], ps_sem.at[cc], pr_sem.at[cc],
            device_id=dev(ep, other_tp), device_id_type=MESH)

    rows = 8 * slots
    for p in range(2):
        for dt, de in peers:
            e, t = peer(dt, de)
            pltpu.make_async_remote_copy(
                sendbuf.at[p], xbuf.at[p, t * 4 + e], xs_sem.at[p, 0], xr_sem.at[p, t * 4 + e],
                device_id=dev(e, t), device_id_type=MESH).wait_recv()

        @pl.loop(0, n_gu)
        def _(j):
            a, b = gu_copy(p, j)
            a.wait()
            b.wait()
            xs = xbuf[p].reshape(rows, xbuf.shape[-1])
            g = jnp.dot(xs, gbuf[j], preferred_element_type=F32)
            u = jnp.dot(xs, ubuf[j], preferred_element_type=F32)
            hbuf[:, pl.ds(pl.multiple_of(j * CW, CW), CW)] = (jax.nn.silu(g) * u).astype(BF16)
            if p == 0:
                a, b = gu_copy(1, j)
                a.start()
                b.start()

        @pl.loop(0, n_cc)
        def _(cc):
            d_copy(p, 2 * cc).wait()
            o = jnp.dot(hbuf[...], dbuf[2 * cc], preferred_element_type=F32)
            obuf[p, 2 * cc] = o.reshape(obuf.shape[2:])
            if p == 0:
                d_copy(1, 2 * cc).start()
            y1_copy(p, cc).start()
            d_copy(p, 2 * cc + 1).wait()
            o = jnp.dot(hbuf[...], dbuf[2 * cc + 1], preferred_element_type=F32)
            obuf[p, 2 * cc + 1] = o.reshape(obuf.shape[2:])
            if p == 0:
                d_copy(1, 2 * cc + 1).start()
            for de in (1, 2, 3):
                x1_copy(p, cc, de, ep).start()
            hx[cc, :, 2 * ep + p] = obuf[p, 2 * cc + 1, :, ep]

    for copy in aux_copies():
        copy.wait_recv()
    build(1, ids_p, gate_p)

    def scatter(which, values):
        v = values.reshape(rows, CW) * gsel[which]
        hi = v.astype(BF16)
        rest = v - hi.astype(F32)
        mid = rest.astype(BF16)
        low = (rest - mid.astype(F32)).astype(BF16)
        s = sel[which]
        return (jnp.dot(s, low, preferred_element_type=F32)
                + jnp.dot(s, mid, preferred_element_type=F32)
                + jnp.dot(s, hi, preferred_element_type=F32))

    @pl.loop(0, n_cc)
    def _(cc):
        for p in range(2):
            y1_copy(p, cc).wait_recv()
            ybuf[p, cc] = ybuf[p, cc] + obuf[p, 2 * cc, tp]
            for de in (1, 2, 3):
                y2_copy(p, cc, de, ep).start()
            hy[cc, 2 * ep + p] = ybuf[p, cc, ep]
        for p in range(2):
            for de in (1, 2, 3):
                x1_copy(p, cc, de, lax.rem(ep + de, 4)).wait_recv()
        psend[cc] = scatter(1, hx[cc, other_tp])
        p_copy(cc).start()
        dacc[cc] = scatter(0, hx[cc, tp])

    @pl.loop(0, n_cc)
    def _(cc):
        for p in range(2):
            for de in (1, 2, 3):
                y2_copy(p, cc, de, lax.rem(ep + de, 4)).wait_recv()
        y_ref[:, pl.ds(pl.multiple_of(2 * cc * CW, CW), CW)] = scatter(0, hy[cc]).astype(y_ref.dtype)
        p_copy(cc).wait_recv()
        y_ref[:, pl.ds(pl.multiple_of((2 * cc + 1) * CW, CW), CW)] = (dacc[cc] + precv[cc]).astype(y_ref.dtype)

    for copy in aux_copies():
        copy.wait_send()
    for p in range(2):
        for i in range(7):
            row_copy(p, i, me).wait_send()

        @pl.loop(0, n_cc)
        def _(cc):
            y1_copy(p, cc).wait_send()
            for de in (1, 2, 3):
                x1_copy(p, cc, de, ep).wait_send()
                y2_copy(p, cc, de, ep).wait_send()

    @pl.loop(0, n_cc)
    def _(cc):
        p_copy(cc).wait_send()


def solution(mesh):
    row_spec = P(('dp', 'ep', 'tp'), None)
    w_in_spec = P('ep', None, 'tp')
    w_out_spec = P('ep', 'tp', None)

    def local_moe(x_local, ids_local, gate_local, w_gate, w_up, w_down):
        n_rows, d_model = x_local.shape
        ff = w_gate.shape[2]
        slots = 2 * n_rows // 8
        n_gu = ff // CW
        n_cc = d_model // CW // 2
        dma = pltpu.SemaphoreType.DMA
        vmem = pl.BlockSpec(memory_space=pltpu.VMEM)
        hbm = pl.BlockSpec(memory_space=pl.ANY)
        return pl.pallas_call(
            moe_kernel,
            out_shape=jax.ShapeDtypeStruct((n_rows, d_model), BF16),
            in_specs=[vmem, vmem, vmem, hbm, hbm, hbm],
            out_specs=vmem,
            scratch_shapes=[
                pltpu.VMEM((n_gu, d_model, CW), BF16),
                pltpu.VMEM((n_gu, d_model, CW), BF16),
                pltpu.VMEM((2 * n_cc, ff, CW), BF16),
                pltpu.VMEM((2, 8, slots, d_model), BF16),
                pltpu.VMEM((8, slots, d_model), BF16),
                pltpu.VMEM((8 * slots, ff), BF16),
                pltpu.VMEM((2, 2 * n_cc, 2, 4, slots, CW), F32),
                pltpu.VMEM((2, n_cc, 4, slots, CW), F32),
                pltpu.VMEM((n_cc, 8, slots, CW), F32),
                pltpu.VMEM((n_cc, 2, 8, slots, CW), F32),
                pltpu.VMEM((n_cc, n_rows, CW), F32),
                pltpu.VMEM((n_cc, n_rows, CW), F32),
                pltpu.VMEM((n_cc, n_rows, CW), F32),
                pltpu.VMEM((2, n_rows), jnp.int32),
                pltpu.VMEM((2, n_rows), F32),
                pltpu.VMEM((2, n_rows, 8 * slots), BF16),
                pltpu.VMEM((2, 8 * slots, CW), F32),
                dma((n_gu,)), dma((n_gu,)), dma((2 * n_cc,)),
                dma((2, 7)), dma((2, 8)), dma((2,)), dma((2,)),
                dma((2, n_cc)), dma((2, n_cc)),
                dma((2, n_cc, 3)), dma((2, n_cc, 4)),
                dma((2, n_cc, 3)), dma((2, n_cc, 4)),
                dma((n_cc,)), dma((n_cc,)),
            ],
            compiler_params=pltpu.CompilerParams(
                collective_id=0, has_side_effects=True, vmem_limit_bytes=60 * 1024 * 1024),
        )(ids_local.T, gate_local.T, x_local, w_gate, w_up, w_down)

    return jax.shard_map(local_moe, mesh=mesh,
                         in_specs=(row_spec, row_spec, row_spec, w_in_spec, w_in_spec, w_out_spec),
                         out_specs=row_spec, check_vma=False)
```

time: 174 us -> 71.4 us (0.41)
  Pallas kernels: 0 us -> 69.3 us
  waiting for transfers between devices: 65 us -> 0 us
  matrix products: 35.7 us -> 0 us
  blocking collectives: 24.4 us -> 0 us
  other arithmetic: 24 us -> 0 us
  between operations: 13.5 us -> 0.01 us
  local copies, waits for them, and re-layouts: 11.3 us -> 1.88 us
    pallas_call x0 -> x1, Pallas kernels: none -> 69.3 us  [local_moe(): pl.pallas_call(moe_kernel, out_shape=jax.ShapeDtypeStruct((n_rows, d_mode...]
    reduce_scatter x1 -> x0, waiting for transfers between devices: 62.4 us -> none  [local_moe(): lax.psum_scatter(partial_sum, ('ep', 'tp'), scatter_dimension=0, tiled=True)]
    dot_general x2 -> x0, matrix products: 35.7 us -> none  [the longest x1 22.5 us: local_moe(): jnp.einsum('ecf,efd->ecd', hidden, w_down, preferred_element_type=jnp.flo...]
    all_gather x2 -> x0, blocking collectives: 24.4 us -> none  [the longest x1 13.6 us: local_moe(): gate_all = lax.all_gather(gate_local, ('ep', 'tp'), tiled=True)]
    scatter-add x1 -> x0, other arithmetic: 12.3 us -> none  [local_moe(): partial_sum = jax.ops.segment_sum(out_rows, tok_rows, num_segments=num_tok)]
    gather x2 -> x0, local copies, waits for them, and re-layouts: 10.3 us -> none  [the longest x1 7.13 us: local_moe(): x_rows = x_all[tok_rows].reshape(e_local, expert_cap, -1)]
    sort x1 -> x0, other arithmetic: 5.04 us -> none  [local_moe(): jnp.argsort(jnp.where(is_local, local_ids, e_local), stable=True)]
    mul x1 -> x0, other arithmetic: 4.5 us -> none  [local_moe(): out_rows = out_rows.reshape(local_pairs, -1) * gate_rows[:, None]]
  transfers between devices with their start and end apart: 2 -> 0, of which waited for: 2 -> 0; matrix products, arithmetic and copies ran while one was open for 5% -> 0% of each run, Pallas kernels for 0% -> 0%
where the time goes in v1:
time: 71.4 us; the launch traced here: 71.2 us
  Pallas kernels  69.3 us (97%)
  local copies, waits for them, and re-layouts  1.88 us (3%)
    pallas_call x1, Pallas kernels, local_moe(): pl.pallas_call(moe_kernel, out_shape=jax.ShapeDtypeStruct((n_rows, d_mode...  69.3 us
    unnamed x1, local copies, waits for them, and re-layouts  1.88 us

profile of v1, /device:TPU:0, one launch (start us, length us, event | category | flops | bytes accessed | tf_op | source)
XLA Modules:
  0.0 71.2 jit_solution(13181068632762361778)
XLA Ops:
  0.0 69.3 %shard_map.64 = bf16[128,2048]{1,0:T(8,128)(2,1)} custom-call(s32[2,128]{1,0:T(2,128)} %bitcast.2, f32[2,128]{1,0:T(2,128)} %bitcast.3, bf16[128,2048]{1,0:T(8,128)(2,1)} %x_ref.1, bf16[2,2048,2816]{2,1,0:T(8,128)(2,1)} %wg_hbm.1, bf16[2,2048,2816]{2,1,0:T(8,128)(2,1)} %wu_hbm.1, bf16[2,2816,2048]{2,1,0:T(8,128)(2,1)} %wd_hbm.1), custom_call_target="tpu_custom_call" | custom-call | tf_op jit(solution)/shard_map/pallas_call | solution.py:248
  69.3 1.9 %copy.8 = bf16[128,2048]{1,0:T(8,128)(2,1)} copy(bf16[128,2048]{1,0:T(8,128)(2,1)} %shard_map.64) | data formatting | bytes 1048576

commit v2 on v0

v2 whole, which is shorter than its diff:
```python
import jax
import jax.numpy as jnp
from jax import lax
from jax.experimental import pallas as pl
from jax.experimental.pallas import tpu as pltpu
from jax.sharding import PartitionSpec as P

MESH = pl.DeviceIdType.MESH
BF16 = jnp.bfloat16
F32 = jnp.float32
CW = 256
NY = 2


def moe_kernel(ids_ref, gate_ref, x_hbm, wg_hbm, wu_hbm, wd_hbm, y_ref,
               xin, gubuf, dbuf, xbuf, sendbuf, hbuf, obuf, ybuf, hy, hx, psend, precv, dacc,
               ids_p, gate_p, sel, gsel,
               xin_sem, gsem, usem, dsem, xs_sem, xr_sem, aux_s, aux_r,
               ys_sem, yr_sem, x1s_sem, x1r_sem, y2s_sem, y2r_sem, ps_sem, pr_sem):
    n_gu = gubuf.shape[0]
    n_c = dbuf.shape[0]
    n_x = n_c - NY
    slots = sendbuf.shape[1]
    rows = 8 * slots
    half = 4 * slots
    ep = lax.axis_index('ep')
    tp = lax.axis_index('tp')
    tq = 1 - tp
    ec = ep + 1 - 2 * lax.rem(ep, 2)
    ex = lax.rem(ep + 2, 4)
    exc = lax.rem(ec + 2, 4)

    def dev(e, t):
        return {'ep': e, 'tp': t}

    def cols(j):
        return pl.ds(pl.multiple_of(j * CW, CW), CW)

    def remote(src, dst, send, recv, e, t):
        return pltpu.make_async_remote_copy(src, dst, send, recv, device_id=dev(e, t), device_id_type=MESH)

    x_copy = pltpu.make_async_copy(x_hbm, xin, xin_sem)
    x_copy.start()

    def gu_copies(p, j):
        return (pltpu.make_async_copy(wg_hbm.at[p, :, cols(j)], gubuf.at[j, :, pl.ds(0, CW)], gsem.at[j]),
                pltpu.make_async_copy(wu_hbm.at[p, :, cols(j)], gubuf.at[j, :, pl.ds(CW, CW)], usem.at[j]))

    def d_copy(p, c):
        return pltpu.make_async_copy(wd_hbm.at[p, :, cols(c)], dbuf.at[c], dsem.at[c])

    def start_gu(p):
        @pl.loop(0, n_gu)
        def _(j):
            for copy in gu_copies(p, j):
                copy.start()

    def start_d(p):
        @pl.loop(0, n_c)
        def _(c):
            d_copy(p, c).start()

    start_gu(0)
    start_d(0)

    barrier = pltpu.get_barrier_semaphore()
    for dt in (0, 1):
        for de in range(4):
            if (dt, de) != (0, 0):
                pl.semaphore_signal(barrier, inc=1, device_id=dev(lax.rem(ep + de, 4), lax.rem(tp + dt, 2)),
                                    device_id_type=MESH)

    def slot_of(ids):
        ids = ids[...]
        e_iota = lax.broadcasted_iota(jnp.int32, (16, 128), 0)
        one0 = jnp.where(e_iota == ids[0:1, :], 1.0, 0.0).astype(F32)
        one1 = jnp.where(e_iota == ids[1:2, :], 1.0, 0.0).astype(F32)
        before = jnp.where(lax.broadcasted_iota(jnp.int32, (128, 128), 0)
                           < lax.broadcasted_iota(jnp.int32, (128, 128), 1), 1.0, 0.0)
        count = jnp.dot((one0 + one1).astype(BF16), before.astype(BF16), preferred_element_type=F32)
        rank0 = jnp.sum(one0 * count, axis=0, keepdims=True).astype(jnp.int32)
        rank1 = jnp.sum(one1 * count, axis=0, keepdims=True).astype(jnp.int32)
        return ids[0:1, :] * slots + rank0, ids[1:2, :] * slots + rank1

    def build(which, ids, gates):
        pos0, pos1 = slot_of(ids)
        k_iota = lax.broadcasted_iota(jnp.int32, (rows, 128), 0)
        hit0 = jnp.where(k_iota == pos0, 1.0, 0.0).astype(F32)
        hit1 = jnp.where(k_iota == pos1, 1.0, 0.0).astype(F32)
        picked = hit0 * gates[0:1, :] + hit1 * gates[1:2, :]
        gsel[which] = jnp.broadcast_to(jnp.sum(picked, axis=1, keepdims=True), (rows, CW))
        both = hit0 + hit1
        sel[which] = both.T.astype(BF16)
        return both.astype(BF16)

    gather = build(0, ids_ref, gate_ref)
    x_copy.wait()
    sorted_rows = jnp.dot(gather, xin[...], preferred_element_type=F32).astype(BF16)
    sendbuf[...] = sorted_rows.reshape(sendbuf.shape)
    for p in range(2):
        xbuf[p, tp, ep] = sendbuf[2 * ep + p]

    pl.semaphore_wait(barrier, 7)

    def row_copy(p, k):
        e, t = ((ex, tp), (exc, tp), (ep, tq), (ec, tq), (ec, tp))[k]
        return remote(sendbuf.at[2 * e + p], xbuf.at[p, tp, ep], xs_sem.at[p, k], xr_sem.at[p, tp, ep], e, t)

    def relay_copy(p, k):
        home = (ex, exc)[k]
        return remote(xbuf.at[p, tp, home], xbuf.at[p, tp, home], xs_sem.at[p, 5 + k], xr_sem.at[p, tp, home],
                      ep, tq)

    def wait_rows(p, th, he):
        remote(sendbuf.at[0], xbuf.at[p, th, he], xs_sem.at[0, 0], xr_sem.at[p, th, he], ep, tq).wait_recv()

    def aux_copies():
        return (remote(ids_ref, ids_p, aux_s.at[0], aux_r.at[0], ep, tq),
                remote(gate_ref, gate_p, aux_s.at[1], aux_r.at[1], ep, tq))

    for k in range(5):
        row_copy(0, k).start()
    for k in (0, 1, 4):
        row_copy(1, k).start()
    for copy in aux_copies():
        copy.start()
    for k in range(2):
        wait_rows(0, tp, (ex, exc)[k])
        relay_copy(0, k).start()
    for k in (2, 3):
        row_copy(1, k).start()
    wait_rows(0, tp, ec)

    def y1_copy(p, cy):
        return remote(obuf.at[p, tq, cy], ybuf.at[p, cy], ys_sem.at[p, cy], yr_sem.at[p, cy], ep, tq)

    def x1_copy(p, g, cx, de, src_ep):
        th = tp + g * (1 - 2 * tp)
        he = lax.rem(ep + de, 4)
        return remote(obuf.at[p, th, NY + cx, he], hx.at[g, cx, 2 * src_ep + p],
                      x1s_sem.at[p, g, cx, de - 1], x1r_sem.at[p, g, cx, src_ep], he, tp)

    def y2_copy(p, cy, de, src_ep):
        he = lax.rem(ep + de, 4)
        return remote(ybuf.at[p, cy, he], hy.at[cy, 2 * src_ep + p],
                      y2s_sem.at[p, cy, de - 1], y2r_sem.at[p, cy, src_ep], he, tp)

    def p_copy(cx):
        return remote(psend.at[cx], precv.at[cx], ps_sem.at[cx], pr_sem.at[cx], ep, tq)

    @pl.loop(0, 4)
    def _(s):
        p = s // 2
        g = lax.rem(s + 1, 4) // 2
        th = tp + g * (1 - 2 * tp)

        @pl.when(s == 1)
        def _():
            for k in range(2):
                wait_rows(1, tp, (ex, exc)[k])
                relay_copy(1, k).start()
            for he in range(4):
                wait_rows(0, tq, he)

        @pl.when(s == 2)
        def _():
            for copy in aux_copies():
                copy.wait_recv()
            build(1, ids_p, gate_p)
            for he in range(4):
                wait_rows(1, tq, he)
            wait_rows(1, tp, ec)

        @pl.when(lax.rem(s, 2) == 0)
        def _():
            @pl.loop(0, n_gu)
            def _(j):
                for copy in gu_copies(p, j):
                    copy.wait()

        xs = xbuf[p, th].reshape(half, xin.shape[1])
        for j in range(n_gu):
            ab = jnp.dot(xs, gubuf[j], preferred_element_type=F32)
            a, b = ab[:, :CW], ab[:, CW:]
            hbuf[:, j * CW:(j + 1) * CW] = (jax.nn.silu(a) * b).astype(BF16)

        @pl.when(s == 1)
        def _():
            start_gu(1)

        @pl.when(lax.rem(s, 2) == 0)
        def _():
            @pl.loop(0, n_c)
            def _(c):
                d_copy(p, c).wait()

        def down(c):
            o = jnp.dot(hbuf[...], dbuf[c], preferred_element_type=F32)
            obuf[p, th, c] = o.reshape(4, slots, CW)

        def send_x(c):
            for de in (2, 3, 1):
                x1_copy(p, g, c - NY, de, ep).start()
            hx[g, c - NY, 2 * ep + p] = obuf[p, th, c, ep]

        for c in range(4):
            down(c)

        @pl.when(g == 1)
        def _():
            for cy in range(NY):
                y1_copy(p, cy).start()

        for c in range(NY, 4):
            send_x(c)
        for c in range(4, n_c):
            down(c)
        for c in range(4, n_c):
            send_x(c)

        @pl.when(s == 1)
        def _():
            start_d(1)

    def scatter(which, values):
        v = values.reshape(rows, CW) * gsel[which]
        hi = v.astype(BF16)
        rest = v - hi.astype(F32)
        mid = rest.astype(BF16)
        low = (rest - mid.astype(F32)).astype(BF16)
        s = sel[which]
        return (jnp.dot(s, low, preferred_element_type=F32)
                + jnp.dot(s, mid, preferred_element_type=F32)
                + jnp.dot(s, hi, preferred_element_type=F32))

    def wait_x(g, cx):
        for p in range(2):
            for de in (1, 2, 3):
                x1_copy(p, g, cx, de, lax.rem(ep + de, 4)).wait_recv()

    def send_p(cx):
        wait_x(1, cx)
        psend[cx] = scatter(1, hx[1, cx])
        p_copy(cx).start()

    send_p(0)
    send_p(1)

    @pl.loop(0, NY)
    def _(cy):
        for p in range(2):
            y1_copy(p, cy).wait_recv()
            ybuf[p, cy] = ybuf[p, cy] + obuf[p, tp, cy]
            for de in (2, 3, 1):
                y2_copy(p, cy, de, ep).start()
            hy[cy, 2 * ep + p] = ybuf[p, cy, ep]

    @pl.loop(2, n_x)
    def _(cx):
        send_p(cx)

    @pl.loop(0, n_x)
    def _(cx):
        wait_x(0, cx)
        dacc[cx] = scatter(0, hx[0, cx])

    @pl.loop(0, n_x - 1)
    def _(cx):
        p_copy(cx).wait_recv()
        y_ref[:, cols(NY + cx)] = (dacc[cx] + precv[cx]).astype(y_ref.dtype)

    @pl.loop(0, NY)
    def _(cy):
        for p in range(2):
            for de in (1, 2, 3):
                y2_copy(p, cy, de, lax.rem(ep + de, 4)).wait_recv()
        y_ref[:, cols(cy)] = scatter(0, hy[cy]).astype(y_ref.dtype)

    p_copy(n_x - 1).wait_recv()
    y_ref[:, cols(n_c - 1)] = (dacc[n_x - 1] + precv[n_x - 1]).astype(y_ref.dtype)

    for copy in aux_copies():
        copy.wait_send()
    for p in range(2):
        for k in range(5):
            row_copy(p, k).wait_send()
        for k in range(2):
            relay_copy(p, k).wait_send()

        @pl.loop(0, NY)
        def _(cy):
            y1_copy(p, cy).wait_send()
            for de in (1, 2, 3):
                y2_copy(p, cy, de, ep).wait_send()

        for g in range(2):
            @pl.loop(0, n_x)
            def _(cx):
                for de in (1, 2, 3):
                    x1_copy(p, g, cx, de, ep).wait_send()

    @pl.loop(0, n_x)
    def _(cx):
        p_copy(cx).wait_send()


def solution(mesh):
    row_spec = P(('dp', 'ep', 'tp'), None)
    w_in_spec = P('ep', None, 'tp')
    w_out_spec = P('ep', 'tp', None)

    def local_moe(x_local, ids_local, gate_local, w_gate, w_up, w_down):
        n_rows, d_model = x_local.shape
        ff = w_gate.shape[2]
        slots = 2 * n_rows // 8
        n_gu = ff // CW
        n_c = d_model // CW
        n_x = n_c - NY
        dma = pltpu.SemaphoreType.DMA
        vmem = pl.BlockSpec(memory_space=pltpu.VMEM)
        hbm = pl.BlockSpec(memory_space=pltpu.HBM)
        return pl.pallas_call(
            moe_kernel,
            out_shape=jax.ShapeDtypeStruct((n_rows, d_model), BF16),
            in_specs=[vmem, vmem, hbm, hbm, hbm, hbm],
            out_specs=vmem,
            scratch_shapes=[
                pltpu.VMEM((n_rows, d_model), BF16),
                pltpu.VMEM((n_gu, d_model, 2 * CW), BF16),
                pltpu.VMEM((n_c, ff, CW), BF16),
                pltpu.VMEM((2, 2, 4, slots, d_model), BF16),
                pltpu.VMEM((8, slots, d_model), BF16),
                pltpu.VMEM((4 * slots, ff), BF16),
                pltpu.VMEM((2, 2, n_c, 4, slots, CW), F32),
                pltpu.VMEM((2, NY, 4, slots, CW), F32),
                pltpu.VMEM((NY, 8, slots, CW), F32),
                pltpu.VMEM((2, n_x, 8, slots, CW), F32),
                pltpu.VMEM((n_x, n_rows, CW), F32),
                pltpu.VMEM((n_x, n_rows, CW), F32),
                pltpu.VMEM((n_x, n_rows, CW), F32),
                pltpu.VMEM((2, n_rows), jnp.int32),
                pltpu.VMEM((2, n_rows), F32),
                pltpu.VMEM((2, n_rows, 8 * slots), BF16),
                pltpu.VMEM((2, 8 * slots, CW), F32),
                dma, dma((n_gu,)), dma((n_gu,)), dma((n_c,)),
                dma((2, 7)), dma((2, 2, 4)), dma((2,)), dma((2,)),
                dma((2, NY)), dma((2, NY)),
                dma((2, 2, n_x, 3)), dma((2, 2, n_x, 4)),
                dma((2, NY, 3)), dma((2, NY, 4)),
                dma((n_x,)), dma((n_x,)),
            ],
            compiler_params=pltpu.CompilerParams(
                collective_id=0, has_side_effects=True, vmem_limit_bytes=52 * 1024 * 1024),
        )(ids_local.T, gate_local.T, x_local, w_gate, w_up, w_down)

    return jax.shard_map(local_moe, mesh=mesh,
                         in_specs=(row_spec, row_spec, row_spec, w_in_spec, w_in_spec, w_out_spec),
                         out_specs=row_spec, check_vma=False)
```

time: 174 us -> 64.3 us (0.37)
  waiting for transfers between devices: 65 us -> 0 us
  Pallas kernels: 0 us -> 61 us
  matrix products: 35.7 us -> 0 us
  blocking collectives: 24.4 us -> 0 us
  other arithmetic: 24 us -> 0 us
  between operations: 13.5 us -> 0.01 us
  local copies, waits for them, and re-layouts: 11.3 us -> 3.19 us
    reduce_scatter x1 -> x0, waiting for transfers between devices: 62.4 us -> none  [local_moe(): lax.psum_scatter(partial_sum, ('ep', 'tp'), scatter_dimension=0, tiled=True)]
    pallas_call x0 -> x1, Pallas kernels: none -> 61 us  [local_moe(): pl.pallas_call(moe_kernel, out_shape=jax.ShapeDtypeStruct((n_rows, d_mode...]
    dot_general x2 -> x0, matrix products: 35.7 us -> none  [the longest x1 22.5 us: local_moe(): jnp.einsum('ecf,efd->ecd', hidden, w_down, preferred_element_type=jnp.flo...]
    all_gather x2 -> x0, blocking collectives: 24.4 us -> none  [the longest x1 13.6 us: local_moe(): gate_all = lax.all_gather(gate_local, ('ep', 'tp'), tiled=True)]
    scatter-add x1 -> x0, other arithmetic: 12.3 us -> none  [local_moe(): partial_sum = jax.ops.segment_sum(out_rows, tok_rows, num_segments=num_tok)]
    gather x2 -> x0, local copies, waits for them, and re-layouts: 10.3 us -> none  [the longest x1 7.13 us: local_moe(): x_rows = x_all[tok_rows].reshape(e_local, expert_cap, -1)]
    sort x1 -> x0, other arithmetic: 5.04 us -> none  [local_moe(): jnp.argsort(jnp.where(is_local, local_ids, e_local), stable=True)]
    mul x1 -> x0, other arithmetic: 4.5 us -> none  [local_moe(): out_rows = out_rows.reshape(local_pairs, -1) * gate_rows[:, None]]
  transfers between devices with their start and end apart: 2 -> 0, of which waited for: 2 -> 0; matrix products, arithmetic and copies ran while one was open for 5% -> 0% of each run, Pallas kernels for 0% -> 0%
where the time goes in v2:
time: 64.3 us; the launch traced here: 64.2 us
  Pallas kernels  61 us (95%)
  local copies, waits for them, and re-layouts  3.19 us (5%)
    pallas_call x1, Pallas kernels, local_moe(): pl.pallas_call(moe_kernel, out_shape=jax.ShapeDtypeStruct((n_rows, d_mode...  61 us
    unnamed x7, local copies, waits for them, and re-layouts  3.19 us

profile of v2, /device:TPU:0, one launch (start us, length us, event | category | flops | bytes accessed | tf_op | source)
XLA Modules:
  0.0 64.2 jit_solution(16673519312968312257)
XLA Ops:
  0.0 0.0 copy-start
  0.0 1.0 %copy-done = bf16[128,2048]{1,0:T(8,128)(2,1)S(1)} copy-done((bf16[128,2048]{1,0:T(8,128)(2,1)S(1)}, bf16[128,2048]{1,0:T(8,128)(2,1)}, u32[]{:S(2)}) %copy-start) | copy-done | bytes 524312
  1.0 0.0 copy-start.1
  1.0 0.7 %copy-done.1 = s32[128,2]{0,1:T(2,128)S(1)} copy-done((s32[128,2]{0,1:T(2,128)S(1)}, s32[128,2]{0,1:T(2,128)}, u32[]{:S(2)}) %copy-start.1) | copy-done | bytes 1048
  1.7 0.0 copy-start.2
  1.7 0.7 %copy-done.2 = f32[128,2]{0,1:T(2,128)S(1)} copy-done((f32[128,2]{0,1:T(2,128)S(1)}, f32[128,2]{0,1:T(2,128)}, u32[]{:S(2)}) %copy-start.2) | copy-done | bytes 1048
  2.4 61.0 %shard_map.64 = bf16[128,2048]{1,0:T(8,128)(2,1)S(1)} custom-call(s32[2,128]{1,0:T(2,128)S(1)} %bitcast.2, f32[2,128]{1,0:T(2,128)S(1)} %bitcast.3, bf16[128,2048]{1,0:T(8,128)(2,1)S(1)} %copy-done, bf16[2,2048,2816]{2,1,0:T(8,128)(2,1)} %wg_hbm.1, bf16[2,2048,2816]{2,1,0:T(8,128)(2,1)} %wu_hbm.1, bf16[2,2816,2048]{2,1,0:T(8,128)(2,1)} %wd_hbm.1), custom_call_target="tpu_custom_call" | custom-call | tf_op jit(solution)/shard_map/pallas_call | solution.py:322
  63.4 0.8 %copy.8 = bf16[128,2048]{1,0:T(8,128)(2,1)} copy(bf16[128,2048]{1,0:T(8,128)(2,1)S(1)} %shard_map.64) | data formatting | bytes 1048576
Async XLA Ops:
  0.0 1.0 %copy-start = (bf16[128,2048]{1,0:T(8,128)(2,1)S(1)}, bf16[128,2048]{1,0:T(8,128)(2,1)}, u32[]{:S(2)}) copy-start(bf16[128,2048]{1,0:T(8,128)(2,1)} %x_hbm.1) | copy-start | bytes 1572868
  1.0 0.7 %copy-start.1 = (s32[128,2]{0,1:T(2,128)S(1)}, s32[128,2]{0,1:T(2,128)}, u32[]{:S(2)}) copy-start(s32[128,2]{0,1:T(2,128)} %param.7) | copy-start | bytes 3076
  1.7 0.7 %copy-start.2 = (f32[128,2]{0,1:T(2,128)S(1)}, f32[128,2]{0,1:T(2,128)}, u32[]{:S(2)}) copy-start(f32[128,2]{0,1:T(2,128)} %param.8) | copy-start | bytes 3076

commit v3 on v2

--- a/solution.py
+++ b/solution.py
@@ -12,11 +12,11 @@
 NY = 2
 
 
-def moe_kernel(ids_ref, gate_ref, x_hbm, wg_hbm, wu_hbm, wd_hbm, y_ref,
-               xin, gubuf, dbuf, xbuf, sendbuf, hbuf, obuf, ybuf, hy, hx, psend, precv, dacc,
+def moe_kernel(ids_hbm, gate_hbm, x_hbm, wg_hbm, wu_hbm, wd_hbm, y_ref,
+               ids_ref, gate_ref, xin, gubuf, dbuf, xbuf, sendbuf, hbuf, obuf, ybuf, hy, hx, psend, precv, dacc,
                ids_p, gate_p, sel, gsel,
-               xin_sem, gsem, usem, dsem, xs_sem, xr_sem, aux_s, aux_r,
-               ys_sem, yr_sem, x1s_sem, x1r_sem, y2s_sem, y2r_sem, ps_sem, pr_sem):
+               in_sem, gu_sem, d_sem, xs_sem, xr_sem, aux_s, aux_r,
+               y1_sem, x1s_sem, x1r_sem, y2s_sem, y2r_sem, ps_sem, pr_sem):
     n_gu = gubuf.shape[0]
     n_c = dbuf.shape[0]
     n_x = n_c - NY
@@ -39,15 +39,17 @@
     def remote(src, dst, send, recv, e, t):
         return pltpu.make_async_remote_copy(src, dst, send, recv, device_id=dev(e, t), device_id_type=MESH)
 
-    x_copy = pltpu.make_async_copy(x_hbm, xin, xin_sem)
-    x_copy.start()
+    in_copies = [pltpu.make_async_copy(src, dst, in_sem.at[i])
+                 for i, (src, dst) in enumerate(((ids_hbm, ids_ref), (gate_hbm, gate_ref), (x_hbm, xin)))]
+    for copy in in_copies:
+        copy.start()
 
     def gu_copies(p, j):
-        return (pltpu.make_async_copy(wg_hbm.at[p, :, cols(j)], gubuf.at[j, :, pl.ds(0, CW)], gsem.at[j]),
-                pltpu.make_async_copy(wu_hbm.at[p, :, cols(j)], gubuf.at[j, :, pl.ds(CW, CW)], usem.at[j]))
+        return (pltpu.make_async_copy(wg_hbm.at[p, :, cols(j)], gubuf.at[j, :, pl.ds(0, CW)], gu_sem),
+                pltpu.make_async_copy(wu_hbm.at[p, :, cols(j)], gubuf.at[j, :, pl.ds(CW, CW)], gu_sem))
 
     def d_copy(p, c):
-        return pltpu.make_async_copy(wd_hbm.at[p, :, cols(c)], dbuf.at[c], dsem.at[c])
+        return pltpu.make_async_copy(wd_hbm.at[p, :, cols(c)], dbuf.at[c], d_sem)
 
     def start_gu(p):
         @pl.loop(0, n_gu)
@@ -64,11 +66,9 @@
     start_d(0)
 
     barrier = pltpu.get_barrier_semaphore()
-    for dt in (0, 1):
-        for de in range(4):
-            if (dt, de) != (0, 0):
-                pl.semaphore_signal(barrier, inc=1, device_id=dev(lax.rem(ep + de, 4), lax.rem(tp + dt, 2)),
-                                    device_id_type=MESH)
+    partners = ((ex, tp), (exc, tp), (ep, tq), (ec, tq), (ec, tp))
+    for e, t in partners:
+        pl.semaphore_signal(barrier, inc=1, device_id=dev(e, t), device_id_type=MESH)
 
     def slot_of(ids):
         ids = ids[...]
@@ -93,26 +93,28 @@
         sel[which] = both.T.astype(BF16)
         return both.astype(BF16)
 
+    in_copies[0].wait()
+    in_copies[1].wait()
     gather = build(0, ids_ref, gate_ref)
-    x_copy.wait()
+    in_copies[2].wait()
     sorted_rows = jnp.dot(gather, xin[...], preferred_element_type=F32).astype(BF16)
     sendbuf[...] = sorted_rows.reshape(sendbuf.shape)
     for p in range(2):
         xbuf[p, tp, ep] = sendbuf[2 * ep + p]
 
-    pl.semaphore_wait(barrier, 7)
+    pl.semaphore_wait(barrier, 5)
 
     def row_copy(p, k):
-        e, t = ((ex, tp), (exc, tp), (ep, tq), (ec, tq), (ec, tp))[k]
-        return remote(sendbuf.at[2 * e + p], xbuf.at[p, tp, ep], xs_sem.at[p, k], xr_sem.at[p, tp, ep], e, t)
+        e, t = partners[k]
+        return remote(sendbuf.at[2 * e + p], xbuf.at[p, tp, ep], xs_sem.at[p], xr_sem.at[p, (1, 2, 0, 0, 3)[k]], e, t)
 
     def relay_copy(p, k):
         home = (ex, exc)[k]
-        return remote(xbuf.at[p, tp, home], xbuf.at[p, tp, home], xs_sem.at[p, 5 + k], xr_sem.at[p, tp, home],
-                      ep, tq)
-
-    def wait_rows(p, th, he):
-        remote(sendbuf.at[0], xbuf.at[p, th, he], xs_sem.at[0, 0], xr_sem.at[p, th, he], ep, tq).wait_recv()
+        return remote(xbuf.at[p, tp, home], xbuf.at[p, tp, home], xs_sem.at[2], xr_sem.at[p, 0], ep, tq)
+
+    def wait_rows(p, k):
+        ref = xbuf.at[p, tq] if k == 0 else xbuf.at[p, tp, (ex, exc, ec)[k - 1]]
+        remote(ref, ref, xs_sem.at[0], xr_sem.at[p, k], ep, tq).wait_recv()
 
     def aux_copies():
         return (remote(ids_ref, ids_p, aux_s.at[0], aux_r.at[0], ep, tq),
@@ -125,28 +127,28 @@
     for copy in aux_copies():
         copy.start()
     for k in range(2):
-        wait_rows(0, tp, (ex, exc)[k])
+        wait_rows(0, 1 + k)
         relay_copy(0, k).start()
     for k in (2, 3):
         row_copy(1, k).start()
-    wait_rows(0, tp, ec)
+    wait_rows(0, 3)
 
     def y1_copy(p, cy):
-        return remote(obuf.at[p, tq, cy], ybuf.at[p, cy], ys_sem.at[p, cy], yr_sem.at[p, cy], ep, tq)
+        return remote(obuf.at[p, tq, cy], ybuf.at[p, cy], y1_sem.at[0], y1_sem.at[1], ep, tq)
 
     def x1_copy(p, g, cx, de, src_ep):
         th = tp + g * (1 - 2 * tp)
         he = lax.rem(ep + de, 4)
         return remote(obuf.at[p, th, NY + cx, he], hx.at[g, cx, 2 * src_ep + p],
-                      x1s_sem.at[p, g, cx, de - 1], x1r_sem.at[p, g, cx, src_ep], he, tp)
+                      x1s_sem, x1r_sem.at[g, cx], he, tp)
 
     def y2_copy(p, cy, de, src_ep):
         he = lax.rem(ep + de, 4)
         return remote(ybuf.at[p, cy, he], hy.at[cy, 2 * src_ep + p],
-                      y2s_sem.at[p, cy, de - 1], y2r_sem.at[p, cy, src_ep], he, tp)
+                      y2s_sem, y2r_sem.at[cy], he, tp)
 
     def p_copy(cx):
-        return remote(psend.at[cx], precv.at[cx], ps_sem.at[cx], pr_sem.at[cx], ep, tq)
+        return remote(psend.at[cx], precv.at[cx], ps_sem, pr_sem.at[cx], ep, tq)
 
     @pl.loop(0, 4)
     def _(s):
@@ -157,26 +159,21 @@
         @pl.when(s == 1)
         def _():
             for k in range(2):
-                wait_rows(1, tp, (ex, exc)[k])
+                wait_rows(1, 1 + k)
                 relay_copy(1, k).start()
-            for he in range(4):
-                wait_rows(0, tq, he)
+            wait_rows(0, 0)
 
         @pl.when(s == 2)
         def _():
             for copy in aux_copies():
                 copy.wait_recv()
             build(1, ids_p, gate_p)
-            for he in range(4):
-                wait_rows(1, tq, he)
-            wait_rows(1, tp, ec)
+            wait_rows(1, 0)
+            wait_rows(1, 3)
 
         @pl.when(lax.rem(s, 2) == 0)
         def _():
-            @pl.loop(0, n_gu)
-            def _(j):
-                for copy in gu_copies(p, j):
-                    copy.wait()
+            pltpu.make_async_copy(gubuf, gubuf, gu_sem).wait()
 
         xs = xbuf[p, th].reshape(half, xin.shape[1])
         for j in range(n_gu):
@@ -190,9 +187,7 @@
 
         @pl.when(lax.rem(s, 2) == 0)
         def _():
-            @pl.loop(0, n_c)
-            def _(c):
-                d_copy(p, c).wait()
+            pltpu.make_async_copy(dbuf, dbuf, d_sem).wait()
 
         def down(c):
             o = jnp.dot(hbuf[...], dbuf[c], preferred_element_type=F32)
@@ -203,7 +198,7 @@
                 x1_copy(p, g, c - NY, de, ep).start()
             hx[g, c - NY, 2 * ep + p] = obuf[p, th, c, ep]
 
-        for c in range(4):
+        for c in range(NY):
             down(c)
 
         @pl.when(g == 1)
@@ -211,12 +206,12 @@
             for cy in range(NY):
                 y1_copy(p, cy).start()
 
-        for c in range(NY, 4):
-            send_x(c)
-        for c in range(4, n_c):
-            down(c)
-        for c in range(4, n_c):
-            send_x(c)
+        mid = (NY + n_c) // 2
+        for part in (range(NY, mid), range(mid, n_c)):
+            for c in part:
+                down(c)
+            for c in part:
+                send_x(c)
 
         @pl.when(s == 1)
         def _():
@@ -234,9 +229,8 @@
                 + jnp.dot(s, hi, preferred_element_type=F32))
 
     def wait_x(g, cx):
-        for p in range(2):
-            for de in (1, 2, 3):
-                x1_copy(p, g, cx, de, lax.rem(ep + de, 4)).wait_recv()
+        six = hx.at[g, cx, pl.ds(0, 6)]
+        remote(six, six, x1s_sem, x1r_sem.at[g, cx], ep, tq).wait_recv()
 
     def send_p(cx):
         wait_x(1, cx)
@@ -246,10 +240,11 @@
     send_p(0)
     send_p(1)
 
+    remote(ybuf, ybuf, y1_sem.at[0], y1_sem.at[1], ep, tq).wait_recv()
+
     @pl.loop(0, NY)
     def _(cy):
         for p in range(2):
-            y1_copy(p, cy).wait_recv()
             ybuf[p, cy] = ybuf[p, cy] + obuf[p, tp, cy]
             for de in (2, 3, 1):
                 y2_copy(p, cy, de, ep).start()
@@ -271,9 +266,8 @@
 
     @pl.loop(0, NY)
     def _(cy):
-        for p in range(2):
-            for de in (1, 2, 3):
-                y2_copy(p, cy, de, lax.rem(ep + de, 4)).wait_recv()
+        six = hy.at[cy, pl.ds(0, 6)]
+        remote(six, six, y2s_sem, y2r_sem.at[cy], ep, tq).wait_recv()
         y_ref[:, cols(cy)] = scatter(0, hy[cy]).astype(y_ref.dtype)
 
     p_copy(n_x - 1).wait_recv()
@@ -282,26 +276,16 @@
     for copy in aux_copies():
         copy.wait_send()
     for p in range(2):
-        for k in range(5):
-            row_copy(p, k).wait_send()
-        for k in range(2):
-            relay_copy(p, k).wait_send()
-
-        @pl.loop(0, NY)
-        def _(cy):
-            y1_copy(p, cy).wait_send()
-            for de in (1, 2, 3):
-                y2_copy(p, cy, de, ep).wait_send()
-
-        for g in range(2):
-            @pl.loop(0, n_x)
-            def _(cx):
-                for de in (1, 2, 3):
-                    x1_copy(p, g, cx, de, ep).wait_send()
-
-    @pl.loop(0, n_x)
-    def _(cx):
-        p_copy(cx).wait_send()
+        five = sendbuf.at[pl.ds(0, 5)]
+        remote(five, five, xs_sem.at[p], xr_sem.at[0, 0], ep, tq).wait_send()
+    four = xbuf.at[0, 0]
+    remote(four, four, xs_sem.at[2], xr_sem.at[0, 0], ep, tq).wait_send()
+    remote(ybuf, ybuf, y1_sem.at[0], y1_sem.at[1], ep, tq).wait_send()
+    sent = hx.at[:, :, pl.ds(0, 6)]
+    remote(sent, sent, x1s_sem, x1r_sem.at[0, 0], ep, tq).wait_send()
+    sent = hy.at[:, pl.ds(0, 6)]
+    remote(sent, sent, y2s_sem, y2r_sem.at[0], ep, tq).wait_send()
+    remote(psend, psend, ps_sem, pr_sem.at[0], ep, tq).wait_send()
 
 
 def solution(mesh):
@@ -322,9 +306,11 @@
         return pl.pallas_call(
             moe_kernel,
             out_shape=jax.ShapeDtypeStruct((n_rows, d_model), BF16),
-            in_specs=[vmem, vmem, hbm, hbm, hbm, hbm],
+            in_specs=[hbm] * 6,
             out_specs=vmem,
             scratch_shapes=[
+                pltpu.VMEM((2, n_rows), jnp.int32),
+                pltpu.VMEM((2, n_rows), F32),
                 pltpu.VMEM((n_rows, d_model), BF16),
                 pltpu.VMEM((n_gu, d_model, 2 * CW), BF16),
                 pltpu.VMEM((n_c, ff, CW), BF16),
@@ -342,16 +328,15 @@
                 pltpu.VMEM((2, n_rows), F32),
                 pltpu.VMEM((2, n_rows, 8 * slots), BF16),
                 pltpu.VMEM((2, 8 * slots, CW), F32),
-                dma, dma((n_gu,)), dma((n_gu,)), dma((n_c,)),
-                dma((2, 7)), dma((2, 2, 4)), dma((2,)), dma((2,)),
-                dma((2, NY)), dma((2, NY)),
-                dma((2, 2, n_x, 3)), dma((2, 2, n_x, 4)),
-                dma((2, NY, 3)), dma((2, NY, 4)),
-                dma((n_x,)), dma((n_x,)),
+                dma((3,)), dma, dma,
+                dma((3,)), dma((2, 4)), dma((2,)), dma((2,)),
+                dma((2,)), dma, dma((2, n_x)),
+                dma, dma((NY,)), dma, dma((n_x,)),
             ],
             compiler_params=pltpu.CompilerParams(
                 collective_id=0, has_side_effects=True, vmem_limit_bytes=52 * 1024 * 1024),
-        )(ids_local.T, gate_local.T, x_local, w_gate, w_up, w_down)
+        )(*(pltpu.with_memory_space_constraint(a, pltpu.HBM) for a in (ids_local.T, gate_local.T, x_local)),
+          w_gate, w_up, w_down)
 
     return jax.shard_map(local_moe, mesh=mesh,
                          in_specs=(row_spec, row_spec, row_spec, w_in_spec, w_in_spec, w_out_spec),

time: 64.3 us -> 59.5 us (0.925)
  Pallas kernels: 61 us -> 58.6 us
  local copies, waits for them, and re-layouts: 3.19 us -> 0.8 us
    unnamed x7 -> x1, local copies, waits for them, and re-layouts: 3.19 us -> 0.8 us
    pallas_call x1, Pallas kernels: 61 us -> 58.6 us  [local_moe(): pl.pallas_call(moe_kernel, out_shape=jax.ShapeDtypeStruct((n_rows, d_mode...]
where the time goes in v3:
time: 59.5 us; the launch traced here: 59.4 us
  Pallas kernels  58.6 us (98%)
  local copies, waits for them, and re-layouts  0.8 us (1%)
    pallas_call x1, Pallas kernels, local_moe(): pl.pallas_call(moe_kernel, out_shape=jax.ShapeDtypeStruct((n_rows, d_mode...  58.6 us

profile of v3, /device:TPU:0, one launch (start us, length us, event | category | flops | bytes accessed | tf_op | source)
XLA Modules:
  0.0 59.4 jit_solution(4897924626980452480)
XLA Ops:
  0.0 58.6 %shard_map.64 = bf16[128,2048]{1,0:T(8,128)(2,1)S(1)} custom-call(s32[2,128]{1,0:T(2,128)} %bitcast.2, f32[2,128]{1,0:T(2,128)} %bitcast.3, bf16[128,2048]{1,0:T(8,128)(2,1)} %x_hbm.1, bf16[2,2048,2816]{2,1,0:T(8,128)(2,1)} %wg_hbm.1, bf16[2,2048,2816]{2,1,0:T(8,128)(2,1)} %wu_hbm.1, bf16[2,2816,2048]{2,1,0:T(8,128)(2,1)} %wd_hbm.1), custom_call_target="tpu_custom_call" | custom-call | tf_op jit(solution)/shard_map/pallas_call | solution.py:306
  58.6 0.8 %copy.8 = bf16[128,2048]{1,0:T(8,128)(2,1)} copy(bf16[128,2048]{1,0:T(8,128)(2,1)S(1)} %shard_map.64) | data formatting | bytes 1048576

commit v4 on v3

--- a/solution.py
+++ b/solution.py
@@ -39,36 +39,47 @@
     def remote(src, dst, send, recv, e, t):
         return pltpu.make_async_remote_copy(src, dst, send, recv, device_id=dev(e, t), device_id_type=MESH)
 
+    barrier = pltpu.get_barrier_semaphore()
+    partners = ((ex, tp), (exc, tp), (ep, tq), (ec, tq), (ec, tp))
+    for e, t in partners:
+        pl.semaphore_signal(barrier, inc=1, device_id=dev(e, t), device_id_type=MESH)
+
     in_copies = [pltpu.make_async_copy(src, dst, in_sem.at[i])
                  for i, (src, dst) in enumerate(((ids_hbm, ids_ref), (gate_hbm, gate_ref), (x_hbm, xin)))]
     for copy in in_copies:
         copy.start()
 
-    def gu_copies(p, j):
-        return (pltpu.make_async_copy(wg_hbm.at[p, :, cols(j)], gubuf.at[j, :, pl.ds(0, CW)], gu_sem),
-                pltpu.make_async_copy(wu_hbm.at[p, :, cols(j)], gubuf.at[j, :, pl.ds(CW, CW)], gu_sem))
-
-    def d_copy(p, c):
-        return pltpu.make_async_copy(wd_hbm.at[p, :, cols(c)], dbuf.at[c], d_sem)
-
-    def start_gu(p):
-        @pl.loop(0, n_gu)
+    def gu_copies(p, j, seg):
+        return (pltpu.make_async_copy(wg_hbm.at[p, :, cols(j)], gubuf.at[j, :, pl.ds(0, CW)], gu_sem.at[seg]),
+                pltpu.make_async_copy(wu_hbm.at[p, :, cols(j)], gubuf.at[j, :, pl.ds(CW, CW)], gu_sem.at[seg]))
+
+    gu_segs = ((0, 4), (4, 8), (8, n_gu))
+    d_segs = ((NY, NY + 1), (NY + 1, n_c), (0, NY))
+
+    def start_gu(p, seg):
+        @pl.loop(*gu_segs[seg])
         def _(j):
-            for copy in gu_copies(p, j):
+            for copy in gu_copies(p, j, seg):
                 copy.start()
 
-    def start_d(p):
-        @pl.loop(0, n_c)
-        def _(c):
-            d_copy(p, c).start()
-
-    start_gu(0)
-    start_d(0)
-
-    barrier = pltpu.get_barrier_semaphore()
-    partners = ((ex, tp), (exc, tp), (ep, tq), (ec, tq), (ec, tp))
-    for e, t in partners:
-        pl.semaphore_signal(barrier, inc=1, device_id=dev(e, t), device_id_type=MESH)
+    def wait_gu(seg):
+        lo, hi = gu_segs[seg]
+        ref = gubuf.at[pl.ds(lo, hi - lo)]
+        pltpu.make_async_copy(ref, ref, gu_sem.at[seg]).wait()
+
+    def start_d(p, seg):
+        for c in range(*d_segs[seg]):
+            pltpu.make_async_copy(wd_hbm.at[p, :, cols(c)], dbuf.at[c], d_sem.at[seg]).start()
+
+    def wait_d(seg):
+        lo, hi = d_segs[seg]
+        ref = dbuf.at[pl.ds(lo, hi - lo)]
+        pltpu.make_async_copy(ref, ref, d_sem.at[seg]).wait()
+
+    for seg in range(3):
+        start_gu(0, seg)
+    for seg in range(3):
+        start_d(0, seg)
 
     def slot_of(ids):
         ids = ids[...]
@@ -137,7 +148,7 @@
         return remote(obuf.at[p, tq, cy], ybuf.at[p, cy], y1_sem.at[0], y1_sem.at[1], ep, tq)
 
     def x1_copy(p, g, cx, de, src_ep):
-        th = tp + g * (1 - 2 * tp)
+        th = tq if g else tp
         he = lax.rem(ep + de, 4)
         return remote(obuf.at[p, th, NY + cx, he], hx.at[g, cx, 2 * src_ep + p],
                       x1s_sem, x1r_sem.at[g, cx], he, tp)
@@ -150,72 +161,65 @@
     def p_copy(cx):
         return remote(psend.at[cx], precv.at[cx], ps_sem, pr_sem.at[cx], ep, tq)
 
-    @pl.loop(0, 4)
-    def _(s):
-        p = s // 2
-        g = lax.rem(s + 1, 4) // 2
-        th = tp + g * (1 - 2 * tp)
-
-        @pl.when(s == 1)
-        def _():
-            for k in range(2):
-                wait_rows(1, 1 + k)
-                relay_copy(1, k).start()
-            wait_rows(0, 0)
-
-        @pl.when(s == 2)
-        def _():
-            for copy in aux_copies():
-                copy.wait_recv()
-            build(1, ids_p, gate_p)
-            wait_rows(1, 0)
-            wait_rows(1, 3)
-
-        @pl.when(lax.rem(s, 2) == 0)
-        def _():
-            pltpu.make_async_copy(gubuf, gubuf, gu_sem).wait()
-
-        xs = xbuf[p, th].reshape(half, xin.shape[1])
-        for j in range(n_gu):
-            ab = jnp.dot(xs, gubuf[j], preferred_element_type=F32)
-            a, b = ab[:, :CW], ab[:, CW:]
-            hbuf[:, j * CW:(j + 1) * CW] = (jax.nn.silu(a) * b).astype(BF16)
-
-        @pl.when(s == 1)
-        def _():
-            start_gu(1)
-
-        @pl.when(lax.rem(s, 2) == 0)
-        def _():
-            pltpu.make_async_copy(dbuf, dbuf, d_sem).wait()
-
-        def down(c):
-            o = jnp.dot(hbuf[...], dbuf[c], preferred_element_type=F32)
+    def gate_up(p, g, wait=False, refill=False):
+        th = tq if g else tp
+        pieces = [(seg,) for seg in range(3)] if refill or (wait and p) else [tuple(range(3))]
+        for piece in pieces:
+            if wait:
+                for seg in piece:
+                    wait_gu(seg)
+            xs = xbuf[p, th].reshape(half, xin.shape[1])
+            for j in range(gu_segs[piece[0]][0], gu_segs[piece[-1]][1]):
+                ab = jnp.dot(xs, gubuf[j], preferred_element_type=F32)
+                a, b = ab[:, :CW], ab[:, CW:]
+                hbuf[g, :, j * CW:(j + 1) * CW] = (jax.nn.silu(a) * b).astype(BF16)
+            if refill:
+                start_gu(1, piece[0])
+
+    def down(p, g, seg, wait=False, refill=False):
+        th = tq if g else tp
+        if wait:
+            wait_d(seg)
+        for c in range(*d_segs[seg]):
+            o = jnp.dot(hbuf[g], dbuf[c], preferred_element_type=F32)
             obuf[p, th, c] = o.reshape(4, slots, CW)
-
-        def send_x(c):
-            for de in (2, 3, 1):
-                x1_copy(p, g, c - NY, de, ep).start()
-            hx[g, c - NY, 2 * ep + p] = obuf[p, th, c, ep]
-
-        for c in range(NY):
-            down(c)
-
-        @pl.when(g == 1)
-        def _():
-            for cy in range(NY):
-                y1_copy(p, cy).start()
-
-        mid = (NY + n_c) // 2
-        for part in (range(NY, mid), range(mid, n_c)):
-            for c in part:
-                down(c)
-            for c in part:
-                send_x(c)
-
-        @pl.when(s == 1)
-        def _():
-            start_d(1)
+            if g and c < NY:
+                y1_copy(p, c).start()
+        for c in range(*d_segs[seg]):
+            if c >= NY:
+                for de in (2, 3, 1):
+                    x1_copy(p, g, c - NY, de, ep).start()
+                hx[g, c - NY, 2 * ep + p] = obuf[p, th, c, ep]
+        if refill:
+            start_d(1, seg)
+
+    gate_up(0, 0, wait=True)
+    for seg in range(3):
+        down(0, 0, seg, wait=True)
+
+    for k in range(2):
+        wait_rows(1, 1 + k)
+        relay_copy(1, k).start()
+    wait_rows(0, 0)
+    gate_up(0, 1, refill=True)
+    for seg in range(3):
+        down(0, 1, seg, refill=True)
+
+    for copy in aux_copies():
+        copy.wait_recv()
+    build(1, ids_p, gate_p)
+    wait_rows(1, 3)
+    gate_up(1, 0, wait=True)
+    down(1, 0, 0, wait=True)
+
+    wait_rows(1, 0)
+    gate_up(1, 1)
+    down(1, 1, 2, wait=True)
+    down(1, 1, 0)
+    down(1, 1, 1, wait=True)
+
+    down(1, 0, 1)
+    down(1, 0, 2)
 
     def scatter(which, values):
         v = values.reshape(rows, CW) * gsel[which]
@@ -316,7 +320,7 @@
                 pltpu.VMEM((n_c, ff, CW), BF16),
                 pltpu.VMEM((2, 2, 4, slots, d_model), BF16),
                 pltpu.VMEM((8, slots, d_model), BF16),
-                pltpu.VMEM((4 * slots, ff), BF16),
+                pltpu.VMEM((2, 4 * slots, ff), BF16),
                 pltpu.VMEM((2, 2, n_c, 4, slots, CW), F32),
                 pltpu.VMEM((2, NY, 4, slots, CW), F32),
                 pltpu.VMEM((NY, 8, slots, CW), F32),
@@ -328,7 +332,7 @@
                 pltpu.VMEM((2, n_rows), F32),
                 pltpu.VMEM((2, n_rows, 8 * slots), BF16),
                 pltpu.VMEM((2, 8 * slots, CW), F32),
-                dma((3,)), dma, dma,
+                dma((3,)), dma((3,)), dma((3,)),
                 dma((3,)), dma((2, 4)), dma((2,)), dma((2,)),
                 dma((2,)), dma, dma((2, n_x)),
                 dma, dma((NY,)), dma, dma((n_x,)),

time: 59.5 us -> 57.9 us (0.973)
  Pallas kernels: 58.6 us -> 57 us
    pallas_call x1, Pallas kernels: 58.6 us -> 57 us  [local_moe(): pl.pallas_call(moe_kernel, out_shape=jax.ShapeDtypeStruct((n_rows, d_mode...]
where the time goes in v4:
time: 57.9 us; the launch traced here: 57.8 us
  Pallas kernels  57 us (98%)
  local copies, waits for them, and re-layouts  0.8 us (1%)
    pallas_call x1, Pallas kernels, local_moe(): pl.pallas_call(moe_kernel, out_shape=jax.ShapeDtypeStruct((n_rows, d_mode...  57 us

profile of v4, /device:TPU:0, one launch (start us, length us, event | category | flops | bytes accessed | tf_op | source)
XLA Modules:
  0.0 57.8 jit_solution(14082807160814249767)
XLA Ops:
  0.0 57.0 %shard_map.64 = bf16[128,2048]{1,0:T(8,128)(2,1)S(1)} custom-call(s32[2,128]{1,0:T(2,128)} %bitcast.2, f32[2,128]{1,0:T(2,128)} %bitcast.3, bf16[128,2048]{1,0:T(8,128)(2,1)} %x_hbm.1, bf16[2,2048,2816]{2,1,0:T(8,128)(2,1)} %wg_hbm.1, bf16[2,2048,2816]{2,1,0:T(8,128)(2,1)} %wu_hbm.1, bf16[2,2816,2048]{2,1,0:T(8,128)(2,1)} %wd_hbm.1), custom_call_target="tpu_custom_call" | custom-call | tf_op jit(solution)/shard_map/pallas_call | solution.py:310
  57.0 0.8 %copy.8 = bf16[128,2048]{1,0:T(8,128)(2,1)} copy(bf16[128,2048]{1,0:T(8,128)(2,1)S(1)} %shard_map.64) | data formatting | bytes 1048576

commit v5 on v4

--- a/solution.py
+++ b/solution.py
@@ -15,18 +15,19 @@
 def moe_kernel(ids_hbm, gate_hbm, x_hbm, wg_hbm, wu_hbm, wd_hbm, y_ref,
                ids_ref, gate_ref, xin, gubuf, dbuf, xbuf, sendbuf, hbuf, obuf, ybuf, hy, hx, psend, precv, dacc,
                ids_p, gate_p, sel, gsel,
-               in_sem, gu_sem, d_sem, xs_sem, xr_sem, aux_s, aux_r,
-               y1_sem, x1s_sem, x1r_sem, y2s_sem, y2r_sem, ps_sem, pr_sem):
+               in_sem, gu_sem, d_sem, out_sem, xr_sem, aux_sem,
+               y1r_sem, x1r_sem, y2r_sem, pr_sem):
     n_gu = gubuf.shape[0]
     n_c = dbuf.shape[0]
     n_x = n_c - NY
-    slots = sendbuf.shape[1]
+    slots = sendbuf.shape[2]
     rows = 8 * slots
     half = 4 * slots
     ep = lax.axis_index('ep')
     tp = lax.axis_index('tp')
     tq = 1 - tp
-    ec = ep + 1 - 2 * lax.rem(ep, 2)
+    core = lax.rem(ep, 2)
+    ec = ep + 1 - 2 * core
     ex = lax.rem(ep + 2, 4)
     exc = lax.rem(ec + 2, 4)
 
@@ -44,7 +45,7 @@
     for e, t in partners:
         pl.semaphore_signal(barrier, inc=1, device_id=dev(e, t), device_id_type=MESH)
 
-    in_copies = [pltpu.make_async_copy(src, dst, in_sem.at[i])
+    in_copies = [pltpu.make_async_copy(src, dst, in_sem.at[i // 2])
                  for i, (src, dst) in enumerate(((ids_hbm, ids_ref), (gate_hbm, gate_ref), (x_hbm, xin)))]
     for copy in in_copies:
         copy.start()
@@ -75,11 +76,6 @@
         lo, hi = d_segs[seg]
         ref = dbuf.at[pl.ds(lo, hi - lo)]
         pltpu.make_async_copy(ref, ref, d_sem.at[seg]).wait()
-
-    for seg in range(3):
-        start_gu(0, seg)
-    for seg in range(3):
-        start_d(0, seg)
 
     def slot_of(ids):
         ids = ids[...]
@@ -102,64 +98,75 @@
         gsel[which] = jnp.broadcast_to(jnp.sum(picked, axis=1, keepdims=True), (rows, CW))
         both = hit0 + hit1
         sel[which] = both.T.astype(BF16)
-        return both.astype(BF16)
-
-    in_copies[0].wait()
-    in_copies[1].wait()
-    gather = build(0, ids_ref, gate_ref)
+
+    def gather_rows(p, pos0, pos1):
+        def place(ids, pos):
+            return jnp.where(lax.rem(ids, 2) == p, pos - (ids // 2 + p) * slots, -1)
+        ids = ids_ref[...]
+        k_iota = lax.broadcasted_iota(jnp.int32, (half, 128), 0)
+        hit0 = jnp.where(k_iota == place(ids[0:1, :], pos0), 1.0, 0.0).astype(F32)
+        hit1 = jnp.where(k_iota == place(ids[1:2, :], pos1), 1.0, 0.0).astype(F32)
+        picked = jnp.dot((hit0 + hit1).astype(BF16), xin[...], preferred_element_type=F32)
+        sendbuf[p] = picked.astype(BF16).reshape(sendbuf.shape[1:])
+
+    two = psend.at[0, pl.ds(0, 2)]
+    pltpu.make_async_copy(two, two, in_sem.at[0]).wait()
+    pos0, pos1 = slot_of(ids_ref)
     in_copies[2].wait()
-    sorted_rows = jnp.dot(gather, xin[...], preferred_element_type=F32).astype(BF16)
-    sendbuf[...] = sorted_rows.reshape(sendbuf.shape)
-    for p in range(2):
-        xbuf[p, tp, ep] = sendbuf[2 * ep + p]
-
+    for seg in range(3):
+        start_gu(0, seg)
+    for seg in range(3):
+        start_d(0, seg)
+    gather_rows(0, pos0, pos1)
     pl.semaphore_wait(barrier, 5)
 
     def row_copy(p, k):
         e, t = partners[k]
-        return remote(sendbuf.at[2 * e + p], xbuf.at[p, tp, ep], xs_sem.at[p], xr_sem.at[p, (1, 2, 0, 0, 3)[k]], e, t)
+        return remote(sendbuf.at[p, e], xbuf.at[p, tp, ep], out_sem, xr_sem.at[p, (1, 2, 0, 0, 2)[k]], e, t)
 
     def relay_copy(p, k):
         home = (ex, exc)[k]
-        return remote(xbuf.at[p, tp, home], xbuf.at[p, tp, home], xs_sem.at[2], xr_sem.at[p, 0], ep, tq)
+        return remote(xbuf.at[p, tp, home], xbuf.at[p, tp, home], out_sem, xr_sem.at[p, 0], ep, tq)
 
     def wait_rows(p, k):
-        ref = xbuf.at[p, tq] if k == 0 else xbuf.at[p, tp, (ex, exc, ec)[k - 1]]
-        remote(ref, ref, xs_sem.at[0], xr_sem.at[p, k], ep, tq).wait_recv()
+        ref = (xbuf.at[p, tq], sendbuf.at[0, 0], sendbuf.at[0, pl.ds(0, 2)])[k]
+        remote(ref, ref, out_sem, xr_sem.at[p, k], ep, tq).wait_recv()
 
     def aux_copies():
-        return (remote(ids_ref, ids_p, aux_s.at[0], aux_r.at[0], ep, tq),
-                remote(gate_ref, gate_p, aux_s.at[1], aux_r.at[1], ep, tq))
+        return (remote(ids_ref, ids_p, aux_sem.at[0], aux_sem.at[1], ep, tq),
+                remote(gate_ref, gate_p, aux_sem.at[0], aux_sem.at[1], ep, tq))
 
     for k in range(5):
         row_copy(0, k).start()
+    gather_rows(1, pos0, pos1)
     for k in (0, 1, 4):
         row_copy(1, k).start()
     for copy in aux_copies():
         copy.start()
+    for p in range(2):
+        xbuf[p, tp, ep] = sendbuf[p, ep]
+    build(0, ids_ref, gate_ref)
     for k in range(2):
         wait_rows(0, 1 + k)
         relay_copy(0, k).start()
     for k in (2, 3):
         row_copy(1, k).start()
-    wait_rows(0, 3)
 
     def y1_copy(p, cy):
-        return remote(obuf.at[p, tq, cy], ybuf.at[p, cy], y1_sem.at[0], y1_sem.at[1], ep, tq)
+        return remote(obuf.at[p, tq, cy], ybuf.at[p, cy], out_sem, y1r_sem, ep, tq)
 
     def x1_copy(p, g, cx, de, src_ep):
         th = tq if g else tp
         he = lax.rem(ep + de, 4)
         return remote(obuf.at[p, th, NY + cx, he], hx.at[g, cx, 2 * src_ep + p],
-                      x1s_sem, x1r_sem.at[g, cx], he, tp)
-
-    def y2_copy(p, cy, de, src_ep):
-        he = lax.rem(ep + de, 4)
+                      out_sem, x1r_sem.at[cx if g else n_x], he, tp)
+
+    def y2_copy(p, cy, he, src_ep):
         return remote(ybuf.at[p, cy, he], hy.at[cy, 2 * src_ep + p],
-                      y2s_sem, y2r_sem.at[cy], he, tp)
-
-    def p_copy(cx):
-        return remote(psend.at[cx], precv.at[cx], ps_sem, pr_sem.at[cx], ep, tq)
+                      out_sem, y2r_sem.at[cy], he, tp)
+
+    def p_copy(cx, last=0):
+        return remote(psend.at[cx], precv.at[cx], out_sem, pr_sem.at[last], ep, tq)
 
     def gate_up(p, g, wait=False, refill=False):
         th = tq if g else tp
@@ -205,10 +212,8 @@
     for seg in range(3):
         down(0, 1, seg, refill=True)
 
-    for copy in aux_copies():
-        copy.wait_recv()
+    remote(two, two, aux_sem.at[0], aux_sem.at[1], ep, tq).wait_recv()
     build(1, ids_p, gate_p)
-    wait_rows(1, 3)
     gate_up(1, 0, wait=True)
     down(1, 0, 0, wait=True)
 
@@ -232,64 +237,86 @@
                 + jnp.dot(s, mid, preferred_element_type=F32)
                 + jnp.dot(s, hi, preferred_element_type=F32))
 
-    def wait_x(g, cx):
-        six = hx.at[g, cx, pl.ds(0, 6)]
-        remote(six, six, x1s_sem, x1r_sem.at[g, cx], ep, tq).wait_recv()
-
-    def send_p(cx):
-        wait_x(1, cx)
+    def wait_x(cx):
+        six = hx.at[1, cx, pl.ds(0, 6)]
+        remote(six, six, out_sem, x1r_sem.at[cx], ep, tq).wait_recv()
+
+    def send_p(cx, last=0):
+        wait_x(cx)
         psend[cx] = scatter(1, hx[1, cx])
-        p_copy(cx).start()
+        if last < 2:
+            p_copy(cx, last).start()
 
     send_p(0)
     send_p(1)
 
-    remote(ybuf, ybuf, y1_sem.at[0], y1_sem.at[1], ep, tq).wait_recv()
+    remote(ybuf, ybuf, out_sem, y1r_sem, ep, tq).wait_recv()
 
     @pl.loop(0, NY)
     def _(cy):
         for p in range(2):
             ybuf[p, cy] = ybuf[p, cy] + obuf[p, tp, cy]
-            for de in (2, 3, 1):
-                y2_copy(p, cy, de, ep).start()
+            for he in (ex - core, ec):
+                y2_copy(p, cy, he, ep).start()
             hy[cy, 2 * ep + p] = ybuf[p, cy, ep]
 
-    @pl.loop(2, n_x)
-    def _(cx):
-        send_p(cx)
+    @pl.loop(0, NY)
+    def _(cy):
+        for p in range(2):
+            y2_copy(p, cy, ex - core + 1, ep).start()
+
+    send_p(2)
+    for cx in range(3, n_x):
+        send_p(cx, 2)
+
+    def send_rest():
+        for cx in range(3, n_x - 1):
+            p_copy(cx, 1).start()
+        p_copy(n_x - 1, 2).start()
+
+    def wait_first():
+        first = precv.at[pl.ds(0, 3)]
+        remote(first, first, out_sem, pr_sem.at[0], ep, tq).wait_recv()
+
+    @pl.when(core == 0)
+    def _():
+        send_rest()
+
+    @pl.when(core == 1)
+    def _():
+        wait_first()
+        send_rest()
+
+    sixes = hx.at[0, :, pl.ds(0, 6)]
+    remote(sixes, sixes, out_sem, x1r_sem.at[n_x], ep, tq).wait_recv()
 
     @pl.loop(0, n_x)
     def _(cx):
-        wait_x(0, cx)
         dacc[cx] = scatter(0, hx[0, cx])
+
+    @pl.when(core == 0)
+    def _():
+        wait_first()
+
+    early = precv.at[pl.ds(3, n_x - 4)]
+    remote(early, early, out_sem, pr_sem.at[1], ep, tq).wait_recv()
 
     @pl.loop(0, n_x - 1)
     def _(cx):
-        p_copy(cx).wait_recv()
         y_ref[:, cols(NY + cx)] = (dacc[cx] + precv[cx]).astype(y_ref.dtype)
 
     @pl.loop(0, NY)
     def _(cy):
         six = hy.at[cy, pl.ds(0, 6)]
-        remote(six, six, y2s_sem, y2r_sem.at[cy], ep, tq).wait_recv()
+        remote(six, six, out_sem, y2r_sem.at[cy], ep, tq).wait_recv()
         y_ref[:, cols(cy)] = scatter(0, hy[cy]).astype(y_ref.dtype)
 
-    p_copy(n_x - 1).wait_recv()
+    p_copy(n_x - 1, 2).wait_recv()
     y_ref[:, cols(n_c - 1)] = (dacc[n_x - 1] + precv[n_x - 1]).astype(y_ref.dtype)
 
-    for copy in aux_copies():
-        copy.wait_send()
-    for p in range(2):
-        five = sendbuf.at[pl.ds(0, 5)]
-        remote(five, five, xs_sem.at[p], xr_sem.at[0, 0], ep, tq).wait_send()
-    four = xbuf.at[0, 0]
-    remote(four, four, xs_sem.at[2], xr_sem.at[0, 0], ep, tq).wait_send()
-    remote(ybuf, ybuf, y1_sem.at[0], y1_sem.at[1], ep, tq).wait_send()
-    sent = hx.at[:, :, pl.ds(0, 6)]
-    remote(sent, sent, x1s_sem, x1r_sem.at[0, 0], ep, tq).wait_send()
-    sent = hy.at[:, pl.ds(0, 6)]
-    remote(sent, sent, y2s_sem, y2r_sem.at[0], ep, tq).wait_send()
-    remote(psend, psend, ps_sem, pr_sem.at[0], ep, tq).wait_send()
+    remote(two, two, aux_sem.at[0], aux_sem.at[1], ep, tq).wait_send()
+    sent = gubuf.at[pl.ds(0, 5), pl.ds(0, 1152)]
+    remote(sent, sent, out_sem, pr_sem.at[0], ep, tq).wait_send()
 
 
 def solution(mesh):
@@ -319,7 +346,7 @@
                 pltpu.VMEM((n_gu, d_model, 2 * CW), BF16),
                 pltpu.VMEM((n_c, ff, CW), BF16),
                 pltpu.VMEM((2, 2, 4, slots, d_model), BF16),
-                pltpu.VMEM((8, slots, d_model), BF16),
+                pltpu.VMEM((2, 4, slots, d_model), BF16),
                 pltpu.VMEM((2, 4 * slots, ff), BF16),
                 pltpu.VMEM((2, 2, n_c, 4, slots, CW), F32),
                 pltpu.VMEM((2, NY, 4, slots, CW), F32),
@@ -332,10 +359,9 @@
                 pltpu.VMEM((2, n_rows), F32),
                 pltpu.VMEM((2, n_rows, 8 * slots), BF16),
                 pltpu.VMEM((2, 8 * slots, CW), F32),
-                dma((3,)), dma((3,)), dma((3,)),
-                dma((3,)), dma((2, 4)), dma((2,)), dma((2,)),
-                dma((2,)), dma, dma((2, n_x)),
-                dma, dma((NY,)), dma, dma((n_x,)),
+                dma((2,)), dma((3,)), dma((3,)),
+                dma, dma((2, 3)), dma((2,)),
+                dma, dma((n_x + 1,)), dma((NY,)), dma((3,)),
             ],
             compiler_params=pltpu.CompilerParams(
                 collective_id=0, has_side_effects=True, vmem_limit_bytes=52 * 1024 * 1024),

time: 57.9 us -> 57.1 us (0.986); the launches traced: 57.8 us -> 56.3 us
  Pallas kernels: 57 us -> 55.5 us
    pallas_call x1, Pallas kernels: 57 us -> 55.5 us  [local_moe(): pl.pallas_call(moe_kernel, out_shape=jax.ShapeDtypeStruct((n_rows, d_mode...]
where the time goes in v5:
time: 57.1 us; the launch traced here: 56.3 us
  Pallas kernels  55.5 us (97%)
  local copies, waits for them, and re-layouts  0.8 us (1%)
    pallas_call x1, Pallas kernels, local_moe(): pl.pallas_call(moe_kernel, out_shape=jax.ShapeDtypeStruct((n_rows, d_mode...  55.5 us

profile of v5, /device:TPU:0, one launch (start us, length us, event | category | flops | bytes accessed | tf_op | source)
XLA Modules:
  0.0 56.3 jit_solution(12978291822279521625)
XLA Ops:
  0.0 55.5 %shard_map.64 = bf16[128,2048]{1,0:T(8,128)(2,1)S(1)} custom-call(s32[2,128]{1,0:T(2,128)} %bitcast.2, f32[2,128]{1,0:T(2,128)} %bitcast.3, bf16[128,2048]{1,0:T(8,128)(2,1)} %x_hbm.1, bf16[2,2048,2816]{2,1,0:T(8,128)(2,1)} %wg_hbm.1, bf16[2,2048,2816]{2,1,0:T(8,128)(2,1)} %wu_hbm.1, bf16[2,2816,2048]{2,1,0:T(8,128)(2,1)} %wd_hbm.1), custom_call_target="tpu_custom_call" | custom-call | tf_op jit(solution)/shard_map/pallas_call | solution.py:337
  55.5 0.8 %copy.8 = bf16[128,2048]{1,0:T(8,128)(2,1)} copy(bf16[128,2048]{1,0:T(8,128)(2,1)S(1)} %shard_map.64) | data formatting | bytes 1048576

commit v6 on v5

--- a/solution.py
+++ b/solution.py
@@ -8,6 +8,8 @@
 MESH = pl.DeviceIdType.MESH
 BF16 = jnp.bfloat16
 F32 = jnp.float32
+F32_MAX = float(jnp.finfo(F32).max)
+BF16_MAX = float(jnp.finfo(BF16).max)
 CW = 256
 NY = 2
 
@@ -227,8 +229,8 @@
     down(1, 0, 2)
 
     def scatter(which, values):
-        v = values.reshape(rows, CW) * gsel[which]
-        hi = v.astype(BF16)
+        v = jnp.clip(values.reshape(rows, CW) * gsel[which], -F32_MAX, F32_MAX)
+        hi = jnp.clip(v, -BF16_MAX, BF16_MAX).astype(BF16)
         rest = v - hi.astype(F32)
         mid = rest.astype(BF16)
         low = (rest - mid.astype(F32)).astype(BF16)

time: 57.1 us -> 57.1 us (level)
  no operation moved by 1% of the time
where the time goes in v6:
time: 57.1 us; the launch traced here: 56.3 us
  Pallas kernels  55.5 us (97%)
  local copies, waits for them, and re-layouts  0.8 us (1%)
    pallas_call x1, Pallas kernels, local_moe(): pl.pallas_call(moe_kernel, out_shape=jax.ShapeDtypeStruct((n_rows, d_mode...  55.5 us

profile of v6, /device:TPU:0, one launch (start us, length us, event | category | flops | bytes accessed | tf_op | source)
XLA Modules:
  0.0 56.3 jit_solution(14692276191190256370)
XLA Ops:
  0.0 55.5 %shard_map.64 = bf16[128,2048]{1,0:T(8,128)(2,1)S(1)} custom-call(s32[2,128]{1,0:T(2,128)} %bitcast.2, f32[2,128]{1,0:T(2,128)} %bitcast.3, bf16[128,2048]{1,0:T(8,128)(2,1)} %x_hbm.1, bf16[2,2048,2816]{2,1,0:T(8,128)(2,1)} %wg_hbm.1, bf16[2,2048,2816]{2,1,0:T(8,128)(2,1)} %wu_hbm.1, bf16[2,2816,2048]{2,1,0:T(8,128)(2,1)} %wd_hbm.1), custom_call_target="tpu_custom_call" | custom-call | tf_op jit(solution)/shard_map/pallas_call | solution.py:339
  55.5 0.8 %copy.8 = bf16[128,2048]{1,0:T(8,128)(2,1)} copy(bf16[128,2048]{1,0:T(8,128)(2,1)S(1)} %shard_map.64) | data formatting | bytes 1048576

commit v7 on v6

--- a/solution.py
+++ b/solution.py
@@ -267,17 +267,16 @@
         for p in range(2):
             y2_copy(p, cy, ex - core + 1, ep).start()
 
-    send_p(2)
-    for cx in range(3, n_x):
+    for cx in range(2, n_x):
         send_p(cx, 2)
 
     def send_rest():
-        for cx in range(3, n_x - 1):
+        for cx in range(2, n_x - 1):
             p_copy(cx, 1).start()
         p_copy(n_x - 1, 2).start()
 
     def wait_first():
-        first = precv.at[pl.ds(0, 3)]
+        first = precv.at[pl.ds(0, 2)]
         remote(first, first, out_sem, pr_sem.at[0], ep, tq).wait_recv()
 
     @pl.when(core == 0)
@@ -300,7 +299,7 @@
     def _():
         wait_first()
 
-    early = precv.at[pl.ds(3, n_x - 4)]
+    early = precv.at[pl.ds(2, n_x - 3)]
     remote(early, early, out_sem, pr_sem.at[1], ep, tq).wait_recv()
 
     @pl.loop(0, n_x - 1)

time: 57.1 us -> 58.4 us (1.023); the launches traced: 56.3 us -> 58.3 us
  Pallas kernels: 55.5 us -> 57.5 us
    pallas_call x1, Pallas kernels: 55.5 us -> 57.5 us  [local_moe(): pl.pallas_call(moe_kernel, out_shape=jax.ShapeDtypeStruct((n_rows, d_mode...]
where the time goes in v7:
time: 58.4 us; the launch traced here: 58.3 us
  Pallas kernels  57.5 us (98%)
  local copies, waits for them, and re-layouts  0.8 us (1%)
    pallas_call x1, Pallas kernels, local_moe(): pl.pallas_call(moe_kernel, out_shape=jax.ShapeDtypeStruct((n_rows, d_mode...  57.5 us

profile of v7, /device:TPU:0, one launch (start us, length us, event | category | flops | bytes accessed | tf_op | source)
XLA Modules:
  0.0 58.3 jit_solution(13510694061919060606)
XLA Ops:
  0.0 57.5 %shard_map.64 = bf16[128,2048]{1,0:T(8,128)(2,1)S(1)} custom-call(s32[2,128]{1,0:T(2,128)} %bitcast.2, f32[2,128]{1,0:T(2,128)} %bitcast.3, bf16[128,2048]{1,0:T(8,128)(2,1)} %x_hbm.1, bf16[2,2048,2816]{2,1,0:T(8,128)(2,1)} %wg_hbm.1, bf16[2,2048,2816]{2,1,0:T(8,128)(2,1)} %wu_hbm.1, bf16[2,2816,2048]{2,1,0:T(8,128)(2,1)} %wd_hbm.1), custom_call_target="tpu_custom_call" | custom-call | tf_op jit(solution)/shard_map/pallas_call | solution.py:338
  57.5 0.8 %copy.8 = bf16[128,2048]{1,0:T(8,128)(2,1)} copy(bf16[128,2048]{1,0:T(8,128)(2,1)S(1)} %shard_map.64) | data formatting | bytes 1048576
